TPU v7x, 32 devices: a whole 2x2x4 slice. The times are simulated.
32 devices in a mesh: row: 4 (over x, core), col: 8 (over z, y).
Axes of the slice: x: 2, y: 2, z: 4, core: 2. Of those that a mesh axis runs over, the one named last changes fastest.
Arguments:
- rhs_c: float32 [12, 512, 6, 1024], P(None, 'row', None, 'col'), may hold values from -6 to 6
- rhs_f: float32 [12, 512, 6, 1024], P(None, 'row', None, 'col'), may hold values from -6 to 6
- pencil_a: bfloat16 [12, 512, 6, 1024], P(None, 'row', None, 'col'), may hold values from -0.5 to 0.5
- pencil_d: bfloat16 [12, 512, 6, 1024], P(None, 'row', None, 'col'), may hold values from -0.5 to 0.5
- pencil_b: bfloat16 [12, 512, 6, 1024], P(None, 'row', None, 'col'), may hold values from -0.5 to 0.5
- pencil_e: bfloat16 [12, 512, 6, 1024], P(None, 'row', None, 'col'), may hold values from -0.5 to 0.5
- d_inverse: float32 [12, 512, 128], P(None, 'row'), may hold values from -0.25 to 2.5
- left_vectors: float32 [12, 512, 128], P(None, 'row'), may hold values from -0.25 to 2.5
- left_inverse: float32 [12, 512, 128], P(None, 'row'), may hold values from -0.25 to 2.5
- left_eigs: float32 [12, 512], P(None, 'row'), may hold values from 1 to 3
- e_inverse: float32 [6, 1024, 128], P(None, 'col'), may hold values from -0.25 to 2.5
- right_vectors: float32 [6, 1024, 128], P(None, 'col'), may hold values from -0.25 to 2.5
- right_inverse: float32 [6, 1024, 128], P(None, 'col'), may hold values from -0.25 to 2.5
- right_eigs: float32 [6, 1024], P(None, 'col'), may hold values from -3 to -1
Outputs:
- updated_c: float32 [12, 512, 6, 1024], P(None, 'row', None, 'col')
- updated_f: float32 [12, 512, 6, 1024], P(None, 'row', None, 'col')
- solved_r: float32 [12, 512, 6, 1024], P(None, 'row', None, 'col')
- solved_l: float32 [12, 512, 6, 1024], P(None, 'row', None, 'col')
All inputs are finite; a program needn't handle non-finite values.
Results may differ from a plain program's by a relative error of at most 0.0003.
Values may be sent and summed in bfloat16 or wider, within the bound.
A program may use at most 128 MiB of HBM per device.

v0:
```python
import jax
import jax.numpy as jnp
from jax import lax
from jax.sharding import PartitionSpec as P

TILE = 128
ORDER = 6144
STEPS = 3


def padded(value, sides, width):
    for axis, dim in sides:
        devices, length = (lax.axis_size(axis), value.shape[dim])
        up = [(i, (i + 1) % devices) for i in range(devices)]
        down = [(j, i) for i, j in up]
        last = lax.slice_in_dim(value, length - width, length, axis=dim)
        initial = lax.slice_in_dim(value, 0, width, axis=dim)
        before = lax.ppermute(last, axis, up)
        after = lax.ppermute(initial, axis, down)
        value = jnp.concatenate([before, value, after], axis=dim)
    return value


def product(left, right):
    return jnp.einsum("bij,bjk->bik", left, right, precision=lax.Precision.HIGHEST)


def solve_tiles(
    a_diag,
    e_diag,
    resid_c,
    resid_f,
    inv_d,
    vec_left,
    back_left,
    eig_left,
    inv_e,
    vec_right,
    back_right,
    eig_right,
):
    coupled = product(a_diag, inv_d)
    merged = product(resid_c - product(coupled, resid_f), inv_e)
    spectral = product(product(back_left, merged), vec_right)
    spectral = spectral / (eig_left[:, :, None] - eig_right[:, None, :])
    new_l = product(product(vec_left, spectral), back_right)
    new_r = product(inv_d, resid_f + product(new_l, e_diag))
    return (new_r, new_l)


def body(
    rhs_c,
    rhs_f,
    pencil_a,
    pencil_d,
    pencil_b,
    pencil_e,
    d_inverse,
    left_vectors,
    left_inverse,
    left_eigs,
    e_inverse,
    right_vectors,
    right_inverse,
    right_eigs,
):
    highest = lax.Precision.HIGHEST
    count_rows = lax.axis_size("row")
    count_cols = lax.axis_size("col")
    this_row = lax.axis_index("row")
    this_col = lax.axis_index("col")
    rows_dev = rhs_c.shape[0]
    cols_dev = rhs_c.shape[2]
    blocks = ORDER // TILE
    local_rows = jnp.arange(rows_dev, dtype=jnp.int32)
    local_cols = jnp.arange(cols_dev, dtype=jnp.int32)
    block_rows = local_rows * count_rows + this_row
    block_cols = local_cols * count_cols + this_col
    near_ad = padded(jnp.stack([pencil_a, pencil_d]), (("col", 4),), TILE)
    near_ad = near_ad.reshape(2, rows_dev, TILE, cols_dev, 3, TILE)
    near_be = padded(jnp.stack([pencil_b, pencil_e]), (("row", 2),), TILE)
    near_be = near_be.reshape(2, rows_dev, 3, TILE, cols_dev, TILE)
    current_c = rhs_c
    current_f = rhs_f
    out_r = jnp.zeros_like(rhs_c)
    out_l = jnp.zeros_like(rhs_c)
    for step in range(STEPS):
        offset = 1 - step
        front_rows = block_cols + offset
        col_valid = (front_rows >= 0) & (front_rows < blocks)
        rows_clip = jnp.clip(front_rows, 0, blocks - 1)
        front_cols = block_rows - offset
        row_valid = (front_cols >= 0) & (front_cols < blocks)
        cols_clip = jnp.clip(front_cols, 0, blocks - 1)
        slot_cols = jnp.clip(rows_clip // count_cols, 0, cols_dev - 1)
        picked_ad = jnp.take(near_ad[:, :, :, :, 1 + offset, :], slot_cols, axis=3)
        panel_a = picked_ad[0]
        panel_d = picked_ad[1]
        slot_rows = jnp.clip(cols_clip // count_rows, 0, rows_dev - 1)
        picked_be = jnp.take(near_be[:, :, 1 - offset, :, :, :], slot_rows, axis=1)
        panel_b = picked_be[0]
        panel_e = picked_be[1]
        owned = col_valid & (rows_clip % count_rows == this_row)
        own_slot = jnp.clip(rows_clip // count_rows, 0, rows_dev - 1)
        resid_c = current_c[own_slot, :, local_cols, :]
        resid_f = current_f[own_slot, :, local_cols, :]
        a_diag = panel_a[own_slot, :, local_cols, :].astype(jnp.float32)
        e_diag = panel_e[own_slot, :, local_cols, :].astype(jnp.float32)
        new_r, new_l = solve_tiles(
            a_diag,
            e_diag,
            resid_c,
            resid_f,
            d_inverse[own_slot],
            left_vectors[own_slot],
            left_inverse[own_slot],
            left_eigs[own_slot],
            e_inverse,
            right_vectors,
            right_inverse,
            right_eigs,
        )
        new_r = jnp.where(owned[:, None, None], new_r, 0.0)
        new_l = jnp.where(owned[:, None, None], new_l, 0.0)
        l_slot = jnp.clip(cols_clip // count_cols, 0, cols_dev - 1)
        front_r = lax.psum(new_r, "row")
        picked = jnp.where((cols_clip % count_cols == this_col)[:, None, None], new_l[l_slot], 0.0)
        front_l = lax.psum(picked, "col")
        front_r = jnp.where(col_valid[:, None, None], front_r, 0.0)
        front_l = jnp.where(row_valid[:, None, None], front_l, 0.0)
        mask_a = (block_rows[:, None] < front_rows[None, :]) & col_valid[None, :]
        term_c = jnp.einsum(
            "apbq,bqs->apbs", panel_a.astype(jnp.float32), front_r, precision=highest
        )
        term_f = jnp.einsum(
            "apbq,bqs->apbs", panel_d.astype(jnp.float32), front_r, precision=highest
        )
        mask_b = (block_cols[None, :] > front_cols[:, None]) & row_valid[:, None]
        gain_c = jnp.einsum(
            "apq,aqbs->apbs", front_l, panel_b.astype(jnp.float32), precision=highest
        )
        gain_f = jnp.einsum(
            "apq,aqbs->apbs", front_l, panel_e.astype(jnp.float32), precision=highest
        )
        wide_a = mask_a[:, None, :, None]
        wide_b = mask_b[:, None, :, None]
        current_c = current_c - jnp.where(wide_a, term_c, 0.0) + jnp.where(wide_b, gain_c, 0.0)
        current_f = current_f - jnp.where(wide_a, term_f, 0.0) + jnp.where(wide_b, gain_f, 0.0)
        place = (owned[None, :] & (local_rows[:, None] == own_slot[None, :]))[:, None, :, None]
        out_r = out_r + jnp.where(place, new_r.transpose(1, 0, 2)[None], 0.0)
        out_l = out_l + jnp.where(place, new_l.transpose(1, 0, 2)[None], 0.0)
    return (current_c, current_f, out_r, out_l)


def solution(mesh):
    in_specs = (
        P(None, "row", None, "col"),
        P(None, "row", None, "col"),
        P(None, "row", None, "col"),
        P(None, "row", None, "col"),
        P(None, "row", None, "col"),
        P(None, "row", None, "col"),
        P(None, "row", None),
        P(None, "row", None),
        P(None, "row", None),
        P(None, "row"),
        P(None, "col", None),
        P(None, "col", None),
        P(None, "col", None),
        P(None, "col"),
    )
    out_specs = (
        P(None, "row", None, "col"),
        P(None, "row", None, "col"),
        P(None, "row", None, "col"),
        P(None, "row", None, "col"),
    )
    return jax.shard_map(body, mesh=mesh, in_specs=in_specs, out_specs=out_specs, check_vma=False)
```

profile of v0, /device:TPU:0, one launch (start us, length us, event | category | flops | bytes accessed | tf_op | source)
XLA Modules:
  0.0 719.9 jit_solution(12369988336342731525)
XLA Ops:
  32.4 6.0 copy.88
  45.1 6.1 copy.91
  88.0 136.5 %collective-permute-done = bf16[2,12,128,6,128]{2,4,3,1,0:T(8,128)(2,1)} collective-permute-done((bf16[2,12,128,6,128]{2,4,3,1,0:T(8,128)(2,1)}, bf16[2,12,128,6,128]{2,4,3,1,0:T(8,128)(2,1)}, u32[]{:S(2)}, u32[]{:S(2)}) %collective-permute-start) | collective-permute-done | bytes 4718624 | tf_op jit(solution)/shard_map/ppermute | solution.py:18
  226.7 6.9 pad_maximum_fusion
  233.7 6.2 fusion.108
  239.9 6.6 copy.83
  246.5 5.8 gather_fusion.27
  272.5 6.9 pad_maximum_fusion.1
  279.5 6.4 slice_bitcast_fusion
  285.9 6.0 gather_fusion.28
  302.4 6.6 copy.93
  309.0 6.0 gather_fusion.29
  320.4 6.7 copy.106
  327.1 5.9 gather_fusion.30
  338.2 6.0 gather_fusion.32
  356.4 5.9 gather_fusion.31
  372.9 14.3 %all-reduce.7.cloned.1.call-done = f32[6,128,128]{2,1,0:T(8,128)} async-done(((f32[6,128,128]{2,1,0:T(8,128)}), f32[6,128,128]{2,1,0:T(8,128)}) %all-reduce.7.cloned.1.call-update) | async-done | bytes 393232 | tf_op jit(solution)/shard_map/psum | solution.py:126
  387.3 10.1 %fusion.11 = f32[12,128,6,128]{1,3,0,2:T(8,128)} fusion(f32[12,128,6,128]{1,3,0,2:T(8,128)} %copy.88, f32[12,128,6,128]{1,3,0,2:T(8,128)} %fusion.31, pred[12,6]{0,1:T(8,128)(4,1)S(1)} %copy-done.48, pred[12,6]{0,1:T(8,128)(4,1)S(1)} %copy-done.49, f32[6,128,128]{2,1,0:T(8,128)} %all-reduce.7.cloned.1.call-done, pred[6]{0:T(512)(128)(4,1)S(1)} %copy-done.65, ...), kind=kOutput, calls=%fused_computation.57 | convolution fusion | flops 1816756224 | bytes 16908438 | tf_op jit(solution)/shard_map/apbq,bqs->apbs/dot_general | solution.py:132
  404.9 7.1 fusion.9
  442.9 55.0 %all-reduce.13.cloned.1.call-done = f32[12,128,128]{2,1,0:T(8,128)} async-done(((f32[12,128,128]{2,1,0:T(8,128)}), f32[12,128,128]{2,1,0:T(8,128)}) %all-reduce.13.cloned.1.call-update) | async-done | bytes 786448 | tf_op jit(solution)/shard_map/psum | solution.py:128
  503.3 29.3 %all-reduce.11.cloned.1.call-done = f32[6,128,128]{2,1,0:T(8,128)} async-done(((f32[6,128,128]{2,1,0:T(8,128)}), f32[6,128,128]{2,1,0:T(8,128)}) %all-reduce.11.cloned.1.call-update) | async-done | bytes 393232 | tf_op jit(solution)/shard_map/psum | solution.py:126
  532.7 10.2 %fusion.7 = f32[12,128,6,128]{1,3,0,2:T(8,128)} fusion(f32[12,128,6,128]{1,3,0,2:T(8,128)} %fusion.11, f32[12,128,6,128]{1,3,0,2:T(8,128)} %fusion.27, pred[12,6]{0,1:T(8,128)(4,1)S(1)} %copy-done.47, pred[12,6]{0,1:T(8,128)(4,1)S(1)} %copy-done.46, f32[6,128,128]{2,1,0:T(8,128)} %all-reduce.11.cloned.1.call-done, pred[6]{0:T(512)(128)(4,1)} %copy-done.50, ...), kind=kOutput, calls=%fused_computation.51 | convolution fusion | flops 1816756224 | bytes 16908944 | tf_op jit(solution)/shard_map/apbq,bqs->apbs/dot_general | solution.py:132
  550.4 7.2 %fusion.5 = f32[12,128,6,128]{1,3,0,2:T(8,128)} fusion(f32[12,128,6,128]{1,3,0,2:T(8,128)} %fusion.9, f32[12,128,6,128]{1,3,0,2:T(8,128)S(1)} %fusion.25, pred[12,6]{0,1:T(8,128)(4,1)S(1)} %copy-done.47, pred[12,6]{0,1:T(8,128)(4,1)S(1)} %copy-done.46, bf16[2,12,128,6,128]{4,2,1,3,0:T(8,128)(2,1)S(1)} %bitcast.225, f32[6,128,128]{2,1,0:T(8,128)S(1)} %copy-done.40, ...), kind=kOutput, calls=%fused_computation.48 | convolution fusion | flops 1816756224 | bytes 16910848 | tf_op jit(solution)/shard_map/apbq,bqs->apbs/dot_general | solution.py:135
  572.0 6.3 select_add_fusion
  578.3 6.1 copy.127
  584.4 6.2 copy.128
  590.7 53.6 %all-reduce.17.cloned.1.call-done = f32[12,128,128]{2,1,0:T(8,128)} async-done(((f32[12,128,128]{2,1,0:T(8,128)}), f32[12,128,128]{2,1,0:T(8,128)}) %all-reduce.17.cloned.1.call-update) | async-done | bytes 786448 | tf_op jit(solution)/shard_map/psum | solution.py:128
  649.5 28.9 %all-reduce.15.cloned.1.call-done = f32[6,128,128]{2,1,0:T(8,128)} async-done(((f32[6,128,128]{2,1,0:T(8,128)}), f32[6,128,128]{2,1,0:T(8,128)}) %all-reduce.15.cloned.1.call-update) | async-done | bytes 393232 | tf_op jit(solution)/shard_map/psum | solution.py:126
  678.4 10.1 %fusion.1 = f32[12,128,6,128]{1,3,0,2:T(8,128)} fusion(f32[12,128,6,128]{1,3,0,2:T(8,128)} %fusion.5, f32[12,128,6,128]{1,3,0,2:T(8,128)} %fusion.21, pred[12,6]{0,1:T(8,128)(4,1)S(1)} %copy-done.45, pred[12,6]{0,1:T(8,128)(4,1)S(1)} %get-tuple-element.34, bf16[2,12,128,6,128]{4,2,1,3,0:T(8,128)(2,1)} %fusion.13, ...), kind=kOutput, calls=%fused_computation.42 | convolution fusion | flops 1816756224 | bytes 16908438 | tf_op jit(solution)/shard_map/apbq,bqs->apbs/dot_general | solution.py:135
  688.5 6.5 copy.126
  697.7 8.8 %fusion.3 = f32[12,128,6,128]{1,3,0,2:T(8,128)} fusion(f32[12,128,6,128]{1,3,0,2:T(8,128)} %fusion.7, f32[12,128,6,128]{1,3,0,2:T(8,128)S(1)} %fusion.23, pred[12,6]{0,1:T(8,128)(4,1)S(1)} %copy-done.45, pred[12,6]{0,1:T(8,128)(4,1)S(1)} %get-tuple-element.34, f32[6,128,128]{2,1,0:T(8,128)S(1)} %copy-done.41, pred[6]{0:T(512)(128)(4,1)S(1)} %copy-done.61, ...), kind=kOutput, calls=%fused_computation.45 | convolution fusion | flops 1816756224 | bytes 16908438 | tf_op jit(solution)/shard_map/apbq,bqs->apbs/dot_general | solution.py:132
  706.5 6.0 copy.125
  (321 shorter events, 207.4 us)
Async XLA Ops:
  7.2 44.0 %copy-start = (f32[12,128,128]{2,1,0:T(8,128)S(1)}, f32[12,128,128]{2,1,0:T(8,128)}, u32[]{:S(2)}) copy-start(f32[12,128,128]{2,1,0:T(8,128)} %param.24) | copy-start | bytes 2359300
  7.2 360.5 %all-reduce.9.cloned.1.call-start = ((), (), s32[]{:S(2)}) async-start(), calls=%async_computation.1 | async-start | bytes 1572864 | tf_op jit(solution)/shard_map/psum | solution.py:128
  19.0 205.5 %collective-permute-start = (bf16[2,12,128,6,128]{2,4,3,1,0:T(8,128)(2,1)}, bf16[2,12,128,6,128]{2,4,3,1,0:T(8,128)(2,1)}, u32[]{:S(2)}, u32[]{:S(2)}) collective-permute-start(bf16[2,12,128,6,128]{2,4,3,1,0:T(8,128)(2,1)} %pad_maximum_fusion.2), channel_id=1, source_target_pairs={{0,1},{1,2},{2,3},{3,4},{4,5},{5,6},{6,7},{7,0},{8,9},{9,10},{10,1... | collective-permute-start | bytes 14155784 | tf_op jit(solution)/shard_map/ppermute | solution.py:18
  22.0 204.7 %collective-permute-start.1 = (bf16[2,12,128,6,128]{2,4,3,1,0:T(8,128)(2,1)}, bf16[2,12,128,6,128]{2,4,3,1,0:T(8,128)(2,1)}, u32[]{:S(2)}, u32[]{:S(2)}) collective-permute-start(bf16[2,12,128,6,128]{2,4,3,1,0:T(8,128)(2,1)} %pad_maximum_fusion.2), channel_id=1, source_target_pairs={{1,0},{2,1},{3,2},{4,3},{5,4},{6,5},{7,6},{0,7},{9,8},{10,9},{11,1... | collective-permute-start | bytes 14155784 | tf_op jit(solution)/shard_map/ppermute | solution.py:19
  27.7 244.8 %collective-permute-start.2 = (bf16[2,12,128,6,128]{4,2,3,1,0:T(8,128)(2,1)}, bf16[2,12,128,6,128]{4,2,3,1,0:T(8,128)(2,1)}, u32[]{:S(2)}, u32[]{:S(2)}) collective-permute-start(bf16[2,12,128,6,128]{4,2,3,1,0:T(8,128)(2,1)} %pad_maximum_fusion.3), channel_id=1, source_target_pairs={{0,8},{8,16},{16,24},{24,0},{1,9},{9,17},{17,25},{25,1},{2,10},{10... | collective-permute-start | bytes 14155784 | tf_op jit(solution)/shard_map/ppermute | solution.py:18
  27.7 244.8 %collective-permute-start.3 = (bf16[2,12,128,6,128]{4,2,3,1,0:T(8,128)(2,1)}, bf16[2,12,128,6,128]{4,2,3,1,0:T(8,128)(2,1)}, u32[]{:S(2)}, u32[]{:S(2)}) collective-permute-start(bf16[2,12,128,6,128]{4,2,3,1,0:T(8,128)(2,1)} %pad_maximum_fusion.3), channel_id=1, source_target_pairs={{8,0},{16,8},{24,16},{0,24},{9,1},{17,9},{25,17},{1,25},{10,2},{18... | collective-permute-start | bytes 14155784 | tf_op jit(solution)/shard_map/ppermute | solution.py:19
  45.1 14.2 %copy-start.42 = (f32[12,128]{1,0:T(8,128)S(1)}, f32[12,128]{1,0:T(8,128)}, u32[]{:S(2)}) copy-start(f32[12,128]{1,0:T(8,128)} %param.27) | copy-start | bytes 18436
  76.0 157.6 %copy-start.66 = (pred[12]{0:T(512)(128)(4,1)}, pred[12]{0:T(512)(128)(4,1)S(1)}, u32[]{:S(2)}) copy-start(pred[12]{0:T(512)(128)(4,1)S(1)} %compare_and_fusion.18) | copy-start | bytes 40
  76.0 157.6 %copy-start.64 = (pred[6]{0:T(512)(128)(4,1)}, pred[6]{0:T(512)(128)(4,1)S(1)}, u32[]{:S(2)}) copy-start(pred[6]{0:T(512)(128)(4,1)S(1)} %compare_and_fusion.20) | copy-start | bytes 22
  78.3 155.3 %copy-start.56 = (pred[6]{0:T(512)(128)(4,1)}, pred[6]{0:T(512)(128)(4,1)S(1)}, u32[]{:S(2)}) copy-start(pred[6]{0:T(512)(128)(4,1)S(1)} %get-tuple-element.55) | copy-start | bytes 22
  78.4 155.3 %copy-start.50 = (pred[6]{0:T(512)(128)(4,1)}, pred[6]{0:T(512)(128)(4,1)S(1)}, u32[]{:S(2)}) copy-start(pred[6]{0:T(512)(128)(4,1)S(1)} %get-tuple-element.57) | copy-start | bytes 22
  78.4 155.3 %copy-start.54 = (pred[6]{0:T(512)(128)(4,1)}, pred[6]{0:T(512)(128)(4,1)S(1)}, u32[]{:S(2)}) copy-start(pred[6]{0:T(512)(128)(4,1)S(1)} %get-tuple-element.56) | copy-start | bytes 22
  78.4 155.3 %copy-start.58 = (pred[12]{0:T(512)(128)(4,1)}, pred[12]{0:T(512)(128)(4,1)S(1)}, u32[]{:S(2)}) copy-start(pred[12]{0:T(512)(128)(4,1)S(1)} %get-tuple-element.44) | copy-start | bytes 40
  78.4 155.3 %copy-start.62 = (pred[12]{0:T(512)(128)(4,1)}, pred[12]{0:T(512)(128)(4,1)S(1)}, u32[]{:S(2)}) copy-start(pred[12]{0:T(512)(128)(4,1)S(1)} %get-tuple-element.45) | copy-start | bytes 40
  79.0 154.7 %copy-start.60 = (pred[6]{0:T(512)(128)(4,1)}, pred[6]{0:T(512)(128)(4,1)S(1)}, u32[]{:S(2)}) copy-start(pred[6]{0:T(512)(128)(4,1)S(1)} %get-tuple-element.53) | copy-start | bytes 22
  302.4 84.9 %all-reduce.7.cloned.1.call-start = ((), (), s32[]{:S(2)}) async-start(), calls=%async_computation | async-start | bytes 786432 | tf_op jit(solution)/shard_map/psum | solution.py:126
  354.2 143.6 %all-reduce.13.cloned.1.call-start = ((), (), s32[]{:S(2)}) async-start(), calls=%async_computation.3 | async-start | bytes 1572864 | tf_op jit(solution)/shard_map/psum | solution.py:128
  367.6 19.6 %copy-start.48 = (pred[12,6]{0,1:T(8,128)(4,1)S(1)}, pred[12,6]{0,1:T(8,128)(4,1)}, u32[]{:S(2)}) copy-start(pred[12,6]{0,1:T(8,128)(4,1)} %get-tuple-element.36) | copy-start | bytes 220
  367.6 19.6 %copy-start.49 = (pred[12,6]{0,1:T(8,128)(4,1)S(1)}, pred[12,6]{0,1:T(8,128)(4,1)}, u32[]{:S(2)}) copy-start(pred[12,6]{0,1:T(8,128)(4,1)} %get-tuple-element.37) | copy-start | bytes 220
  367.6 19.6 %copy-start.65 = (pred[6]{0:T(512)(128)(4,1)S(1)}, pred[6]{0:T(512)(128)(4,1)}, u32[]{:S(2)}) copy-start(pred[6]{0:T(512)(128)(4,1)} %copy-done.64) | copy-start | bytes 22
  426.0 71.9 %copy-start.11 = (bf16[12,128,6,128]{3,1,2,0:T(8,128)(2,1)S(1)}, bf16[12,128,6,128]{3,1,2,0:T(8,128)(2,1)}, u32[]{:S(2)}) copy-start(bf16[12,128,6,128]{3,1,2,0:T(8,128)(2,1)} %get-tuple-element.27) | copy-start | bytes 7077892
  441.8 90.8 %copy-start.46 = (pred[12,6]{0,1:T(8,128)(4,1)S(1)}, pred[12,6]{0,1:T(8,128)(4,1)}, u32[]{:S(2)}) copy-start(pred[12,6]{0,1:T(8,128)(4,1)} %get-tuple-element.32) | copy-start | bytes 220
  441.8 90.8 %copy-start.47 = (pred[12,6]{0,1:T(8,128)(4,1)S(1)}, pred[12,6]{0,1:T(8,128)(4,1)}, u32[]{:S(2)}) copy-start(pred[12,6]{0,1:T(8,128)(4,1)} %get-tuple-element.33) | copy-start | bytes 220
  441.8 90.8 %all-reduce.11.cloned.1.call-start = ((), (), s32[]{:S(2)}) async-start(), calls=%async_computation.2 | async-start | bytes 786432 | tf_op jit(solution)/shard_map/psum | solution.py:126
  442.9 201.3 %all-reduce.17.cloned.1.call-start = ((), (), s32[]{:S(2)}) async-start(), calls=%async_computation.5 | async-start | bytes 1572864 | tf_op jit(solution)/shard_map/psum | solution.py:128
  532.7 13.2 %copy-start.63 = (pred[12]{0:T(512)(128)(4,1)S(1)}, pred[12]{0:T(512)(128)(4,1)}, u32[]{:S(2)}) copy-start(pred[12]{0:T(512)(128)(4,1)} %copy-done.62) | copy-start | bytes 40
  571.7 106.7 %all-reduce.15.cloned.1.call-start = ((), (), s32[]{:S(2)}) async-start(), calls=%async_computation.4 | async-start | bytes 786432 | tf_op jit(solution)/shard_map/psum | solution.py:126
  584.4 59.8 %copy-start.5 = (bf16[12,128,6,128]{3,1,2,0:T(8,128)(2,1)S(1)}, bf16[12,128,6,128]{3,1,2,0:T(8,128)(2,1)}, u32[]{:S(2)}) copy-start(bf16[12,128,6,128]{3,1,2,0:T(8,128)(2,1)} %get-tuple-element.24) | copy-start | bytes 7077892
  584.4 59.8 %copy-start.59 = (pred[12]{0:T(512)(128)(4,1)S(1)}, pred[12]{0:T(512)(128)(4,1)}, u32[]{:S(2)}) copy-start(pred[12]{0:T(512)(128)(4,1)} %copy-done.58) | copy-start | bytes 40
  590.6 87.8 %copy-start.45 = (pred[12,6]{0,1:T(8,128)(4,1)S(1)}, pred[12,6]{0,1:T(8,128)(4,1)}, u32[]{:S(2)}) copy-start(pred[12,6]{0,1:T(8,128)(4,1)} %get-tuple-element.35) | copy-start | bytes 220
  590.6 87.8 %copy-start.61 = (pred[6]{0:T(512)(128)(4,1)S(1)}, pred[6]{0:T(512)(128)(4,1)}, u32[]{:S(2)}) copy-start(pred[6]{0:T(512)(128)(4,1)} %copy-done.60) | copy-start | bytes 22
  697.7 14.8 %copy-start.1 = (f32[12,128,128]{2,1,0:T(8,128)S(1)}, f32[12,128,128]{2,1,0:T(8,128)}, u32[]{:S(2)}) copy-start(f32[12,128,128]{2,1,0:T(8,128)} %param.24) | copy-start | bytes 2359300
  (62 other events, 431.7 us)
Sparse Core Ops, SparseCore 0:
  272.6 75.0 all-reduce.8
  354.4 32.8 all-reduce.6
  422.7 75.0 all-reduce.12
  500.7 31.9 all-reduce.10
  569.1 75.0 all-reduce.16
  646.4 31.9 all-reduce.14
where the time goes:
time: 731 us; the launch traced here: 720 us
  waiting for transfers between devices  320 us (44%)
  local copies, waits for them, and re-layouts  194 us (27%)
  matrix products  112 us (15%)
  other arithmetic  70 us (10%)
  between operations  16 us (2%)
  starting transfers between devices  8.39 us (1%)
    ppermute x2, waiting for transfers between devices, padded(): before = lax.ppermute(last, axis, up)  137 us
    psum x3, waiting for transfers between devices, body(): front_l = lax.psum(picked, 'col')  109 us
    psum x3, waiting for transfers between devices, body(): front_r = lax.psum(new_r, 'row')  72.6 us
    unnamed x176, local copies, waits for them, and re-layouts  49.8 us
    dot_general x27, matrix products, product(): jnp.einsum('bij,bjk->bik', left, right, precision=lax.Precision.HIGHEST)  30.8 us
    dot_general x3, matrix products, body(): jnp.einsum('apbq,bqs->apbs', panel_a.astype(jnp.float32), front_r, precis...  29.1 us
    slice x4, local copies, waits for them, and re-layouts, body(): picked_ad = jnp.take(near_ad[:, :, :, :, 1 + offset, :], slot_cols, axis=3)  26.2 us
    dot_general x3, matrix products, body(): jnp.einsum('apbq,bqs->apbs', panel_d.astype(jnp.float32), front_r, precis...  24.4 us
  transfers between devices with their start and end apart: 10, of which 7 were waited for; matrix products, arithmetic and copies ran while one was open for 35% of the time, Pallas kernels for 0%

commit v1 on v0

v1 whole, which is shorter than its diff:
```python
import functools

import jax
import jax.numpy as jnp
from jax import lax
from jax.experimental import pallas as pl
from jax.experimental.pallas import tpu as pltpu
from jax.sharding import PartitionSpec as P

TILE = 128
PIECES = 3


def product(left, right):
    return jnp.einsum("bij,bjk->bik", left, right, precision=lax.Precision.HIGHEST)


def half_product(exact, value):
    hi, lo = split(value)
    dot = functools.partial(jnp.einsum, "bij,bjk->bik", preferred_element_type=jnp.float32)
    return dot(exact, hi) + dot(exact, lo)


def product_half(value, exact):
    hi, lo = split(value)
    dot = functools.partial(jnp.einsum, "bij,bjk->bik", preferred_element_type=jnp.float32)
    return dot(hi, exact) + dot(lo, exact)


def split(value):
    hi = lax.reduce_precision(value, 8, 7)
    return hi.astype(jnp.bfloat16), (value - hi).astype(jnp.bfloat16)


def heights(rows_dev, cols_dev, count_rows, count_cols):
    return [min(rows_dev, (b * count_cols + count_cols - 1) // count_rows + 1) for b in range(cols_dev)]


def pack(left, right, tall):
    tiles = [jnp.stack([left[:n, b], right[:n, b]]) for b, n in enumerate(tall)]
    return jnp.concatenate(tiles, axis=1)


def update_kernel(
    count_rows, count_cols, place, c_ref, f_ref, a_ref, d_ref, b_ref, e_ref, r_ref, l_ref, ad_ref, be_ref, c_out, f_out
):
    a = pl.program_id(0)
    row, col = place[0], place[1]
    cols_dev = c_ref.shape[1]
    total = ad_ref.shape[2]
    i = a * count_rows + row
    col_side, row_side = lax.rem(col, 2), lax.rem(row, 2)
    for b in range(cols_dev):
        j = b * count_cols + col

        @pl.when(i > j)
        def _():
            c_out[0, b] = c_ref[0, b]
            f_out[0, b] = f_ref[0, b]

        @pl.when(i <= j)
        def _():
            slot_right = jnp.minimum(b + (col == count_cols - 1).astype(jnp.int32), cols_dev - 1)
            slot_left = jnp.maximum(b - (col == 0).astype(jnp.int32), 0)
            right = jnp.clip(place[2 + slot_right] + a, 0, total - 1)
            left = jnp.clip(place[2 + slot_left] + a, 0, total - 1)
            up = jnp.clip(place[2 + b] + a - (row == 0).astype(jnp.int32), 0, total - 1)
            down = jnp.clip(place[2 + b] + a + (row == count_rows - 1).astype(jnp.int32), 0, total - 1)
            keep_mid = jnp.full((TILE, TILE), jnp.where(i < j, 1.0, 0.0), jnp.float32).astype(jnp.bfloat16)
            keep_far = jnp.full((TILE, TILE), jnp.where(i < j - 1, 1.0, 0.0), jnp.float32).astype(jnp.bfloat16)

            def wide(which, own):
                return jnp.concatenate(
                    [ad_ref[col_side, which, right], own * keep_mid, ad_ref[1 - col_side, which, left] * keep_far], axis=1
                )

            lhs = jnp.concatenate([wide(0, a_ref[0, b]), wide(1, d_ref[0, b])], axis=0)
            first = jnp.dot(lhs, r_ref[b], preferred_element_type=jnp.float32)

            def tall(which, own):
                return jnp.concatenate(
                    [be_ref[1 - row_side, which, up], own * keep_mid, be_ref[row_side, which, down] * keep_far], axis=0
                )

            rhs = jnp.concatenate([tall(0, b_ref[0, b]), tall(1, e_ref[0, b])], axis=1)
            second = jnp.dot(l_ref[0], rhs, preferred_element_type=jnp.float32)
            c_out[0, b] = (
                c_ref[0, b]
                - (first[:TILE, :TILE] + first[:TILE, TILE:])
                + (second[:TILE, :TILE] + second[TILE:, :TILE])
            )
            f_out[0, b] = (
                f_ref[0, b]
                - (first[TILE:, :TILE] + first[TILE:, TILE:])
                + (second[:TILE, TILE:] + second[TILE:, TILE:])
            )


def body(
    rhs_c,
    rhs_f,
    pencil_a,
    pencil_d,
    pencil_b,
    pencil_e,
    d_inverse,
    left_vectors,
    left_inverse,
    left_eigs,
    e_inverse,
    right_vectors,
    right_inverse,
    right_eigs,
):
    count_rows = lax.axis_size("row")
    count_cols = lax.axis_size("col")
    row = lax.axis_index("row")
    col = lax.axis_index("col")
    c, f, a, d, b, e = [
        x.transpose(0, 2, 1, 3) for x in (rhs_c, rhs_f, pencil_a, pencil_d, pencil_b, pencil_e)
    ]
    rows_dev, cols_dev = c.shape[:2]
    blocks = rows_dev * count_rows
    slots = jnp.arange(cols_dev, dtype=jnp.int32)
    block_cols = slots * count_cols + col
    tall = heights(rows_dev, cols_dev, count_rows, count_cols)
    offsets = [sum(tall[:k]) for k in range(cols_dev)]

    def shift(value, axis, by):
        n = lax.axis_size(axis)
        return lax.ppermute(value, axis, [(k, (k + by) % n) for k in range(n)])

    band = jnp.clip((block_cols - row) // count_rows, 0, rows_dev - 1)
    band_ad = jnp.stack([a[band, slots], d[band, slots]])
    band_be = jnp.stack([b[band, slots], e[band, slots]])
    from_right = shift(band_ad, "col", -1)
    from_left = shift(band_ad[0], "col", 1)
    from_up = shift(band_be, "row", 1)
    from_down = shift(band_be[1], "row", -1)
    from_right = jnp.where(col == count_cols - 1, jnp.roll(from_right, -1, axis=1), from_right)
    from_left = jnp.where(col == 0, jnp.roll(from_left, 1, axis=0), from_left)

    pack_ad = pack(a, d, tall)
    pack_be = pack(b, e, tall)
    total = pack_ad.shape[1]
    pieces = min(PIECES, total)
    cuts = [total * k // pieces for k in range(pieces + 1)]
    swap_col = [(k, k ^ 1) for k in range(count_cols)]
    relay_col = [(k, (k + 2 if k % 2 == 0 else k - 2) % count_cols) for k in range(count_cols)]
    swap_row = [(k, k ^ 1) for k in range(count_rows)]
    cross_row = [(k, (k - 1 if k % 2 == 0 else k + 1) % count_rows) for k in range(count_rows)]
    swapped, relayed = [], []
    for lo, hi in zip(cuts[:-1], cuts[1:]):
        got = lax.ppermute(pack_ad[:, lo:hi], "col", swap_col)
        swapped.append(got)
        relayed.append(lax.ppermute(got, "col", relay_col))
    be_swap = lax.ppermute(pack_be, "row", swap_row)
    be_cross = lax.ppermute(pack_be, "row", cross_row)
    near_ad = jnp.stack([jnp.concatenate(swapped, axis=1), jnp.concatenate(relayed, axis=1)])
    near_be = jnp.stack([be_swap, be_cross])

    phase = (col - row) % count_rows
    ahead = phase == count_rows - 1
    level = phase == 0
    behind = phase == 1
    mine = (block_cols + 1 - row) // count_rows
    front_rows = mine * count_rows + row
    valid = (ahead | level | behind) & (front_rows >= 0) & (front_rows < blocks)
    mine = jnp.clip(mine, 0, rows_dev - 1)
    front_c = c[mine, slots]
    front_f = f[mine, slots]
    own_a, own_d, own_b, own_e = [x[mine, slots] for x in (a, d, b, e)]
    a_diag = jnp.where(ahead, from_right[0], jnp.where(level, own_a, from_left)).astype(jnp.float32)
    e_diag = jnp.where(ahead, from_up[1], jnp.where(level, own_e, from_down)).astype(jnp.float32)
    inv_d, vec_left, back_left = d_inverse[mine], left_vectors[mine], left_inverse[mine]
    spread = left_eigs[mine][:, :, None] - right_eigs[:, None, :]
    coupled = product(a_diag, inv_d)

    def solve(resid_c, resid_f):
        merged = product(resid_c - product(coupled, resid_f), e_inverse)
        spectral = product(product(back_left, merged), right_vectors) / spread
        new_l = product(product(vec_left, spectral), right_inverse)
        new_r = product(inv_d, resid_f + product(new_l, e_diag))
        keep = valid[:, None, None]
        return jnp.where(keep, new_r, 0.0), jnp.where(keep, new_l, 0.0)

    def onward(value, by):
        got = shift(value, "col", by)
        moved = jnp.concatenate([jnp.zeros_like(got[:1]), got[:-1]])
        return jnp.where(col < by, moved, got)

    r_one, l_one = solve(front_c, front_f)
    r_in, l_in = shift(r_one, "row", -1), onward(l_one, 1)
    r_far, l_far = shift(r_one, "row", -2), onward(l_one, 2)
    r_two, l_two = solve(
        front_c - half_product(from_right[0], r_in) + product_half(l_in, from_up[0]),
        front_f - half_product(from_right[1], r_in) + product_half(l_in, from_up[1]),
    )
    base_c = front_c - half_product(from_right[0], r_far) + product_half(l_far, from_up[0])
    base_f = front_f - half_product(from_right[1], r_far) + product_half(l_far, from_up[1])
    r_in, l_in = shift(r_two, "row", -1), onward(l_two, 1)
    r_three, l_three = solve(
        base_c - half_product(own_a, r_in) + product_half(l_in, own_b),
        base_f - half_product(own_d, r_in) + product_half(l_in, own_e),
    )
    new_r = jnp.where(ahead, r_one, jnp.where(level, r_two, r_three))
    new_l = jnp.where(ahead, l_one, jnp.where(level, l_two, l_three))

    every_r = lax.all_gather(new_r, "row")
    every_l = lax.all_gather(new_l, "col")
    r_parts, l_parts = [], []
    block_rows = jnp.arange(rows_dev, dtype=jnp.int32) * count_rows + row
    for offset in (1, 0, -1):
        r_parts.append(every_r[(col + offset) % count_rows])
        at = block_rows - offset
        inside = (at >= 0) & (at < blocks)
        at = jnp.clip(at, 0, blocks - 1)
        l_parts.append(jnp.where(inside[:, None, None], every_l[at % count_cols, at // count_cols], 0.0))
    r_all = jnp.concatenate(split(jnp.concatenate(r_parts, axis=1)), axis=2)
    l_all = jnp.concatenate(split(jnp.concatenate(l_parts, axis=2)), axis=1)

    place = jnp.concatenate([jnp.stack([row, col]).astype(jnp.int32), jnp.array(offsets, jnp.int32)])
    line = pl.BlockSpec((1, cols_dev, TILE, TILE), lambda k: (k, 0, 0, 0))
    whole = pl.BlockSpec(memory_space=pltpu.VMEM)
    new_c, new_f = pl.pallas_call(
        functools.partial(update_kernel, count_rows, count_cols),
        grid=(rows_dev,),
        in_specs=[pl.BlockSpec(memory_space=pltpu.SMEM)]
        + [line] * 6
        + [whole, pl.BlockSpec((1, 2 * TILE, 3 * TILE), lambda k: (k, 0, 0)), whole, whole],
        out_specs=[line, line],
        out_shape=[jax.ShapeDtypeStruct(c.shape, jnp.float32)] * 2,
        compiler_params=pltpu.CompilerParams(vmem_limit_bytes=48 * 1024 * 1024),
        name="update",
    )(place, c, f, a, d, b, e, r_all, l_all, near_ad, near_be)

    here = (valid[None, :] & (jnp.arange(rows_dev, dtype=jnp.int32)[:, None] == mine[None, :]))[:, :, None, None]
    out_r = jnp.where(here, new_r[None], 0.0)
    out_l = jnp.where(here, new_l[None], 0.0)
    return tuple(x.transpose(0, 2, 1, 3) for x in (new_c, new_f, out_r, out_l))


def solution(mesh):
    grid = P(None, "row", None, "col")
    left, right = P(None, "row", None), P(None, "col", None)
    in_specs = (grid,) * 6 + (left,) * 3 + (P(None, "row"),) + (right,) * 3 + (P(None, "col"),)
    return jax.shard_map(body, mesh=mesh, in_specs=in_specs, out_specs=(grid,) * 4, check_vma=False)
```

time: 731 us -> 332 us (0.45); the launches traced: 720 us -> 330 us
  waiting for transfers between devices: 320 us -> 114 us
  local copies, waits for them, and re-layouts: 194 us -> 92.3 us
  matrix products: 112 us -> 33.1 us
  other arithmetic: 70 us -> 36.3 us
  Pallas kernels: 0 us -> 21.2 us
  starting transfers between devices: 8.39 us -> 17.6 us
    psum x6 -> x0, waiting for transfers between devices: 181 us -> none  [the longest x3 109 us: body(): front_l = lax.psum(picked, 'col')]
    dot_general x12 -> x24, matrix products: 80.8 us -> 16.5 us  [the longest x12 9.98 us: product_half(): return dot(hi, exact) + dot(lo, exact)]
    gather x33 -> x17, local copies, waits for them, and re-layouts: 94.5 us -> 46.6 us  [the longest x4 11.8 us: body(): own_a, own_d, own_b, own_e = [x[mine, slots] for x in (a, d, b, e)]]
    unnamed x176 -> x82, local copies, waits for them, and re-layouts: 49.8 us -> 13.7 us
    another operation x0 -> x24, local copies, waits for them, and re-layouts: none -> 26.1 us  [pack(): tiles = [jnp.stack([left[:n, b], right[:n, b]]) for b, n in enumerate(tall)]]
    ppermute x4 -> x18, waiting for transfers between devices: 139 us -> 114 us  [the longest x3 80.1 us: body(): got = lax.ppermute(pack_ad[:, lo:hi], 'col', swap_col)]
    slice x4 -> x7, local copies, waits for them, and re-layouts: 26.2 us -> 4.62 us  [the longest x2 1.89 us: body(): jnp.roll(from_right, -1, axis=1)]
    pallas_call x0 -> x1, Pallas kernels: none -> 21.2 us  [body(): pl.pallas_call(functools.partial(update_kernel, count_rows, count_cols),...]
  transfers between devices with their start and end apart: 10 -> 20, of which waited for: 7 -> 7; matrix products, arithmetic and copies ran while one was open for 35% -> 39% of each run, Pallas kernels for 0% -> 0%
where the time goes in v1:
time: 332 us; the launch traced here: 330 us
  waiting for transfers between devices  114 us (34%)
  local copies, waits for them, and re-layouts  92.3 us (28%)
  other arithmetic  36.3 us (11%)
  matrix products  33.1 us (10%)
  Pallas kernels  21.2 us (6%)
  starting transfers between devices  17.6 us (5%)
  between operations  15.2 us (5%)
    ppermute x3, waiting for transfers between devices, body(): got = lax.ppermute(pack_ad[:, lo:hi], 'col', swap_col)  80.1 us
    another operation x24, local copies, waits for them, and re-layouts, pack(): tiles = [jnp.stack([left[:n, b], right[:n, b]]) for b, n in enumerate(tall)]  26.1 us
    ppermute x3, waiting for transfers between devices, body(): relayed.append(lax.ppermute(got, 'col', relay_col))  25.9 us
    pallas_call x1, Pallas kernels, body(): pl.pallas_call(functools.partial(update_kernel, count_rows, count_cols),...  21.2 us
    dot_general x25, matrix products, product(): jnp.einsum('bij,bjk->bik', left, right, precision=lax.Precision.HIGHEST)  16.6 us
    unnamed x82, local copies, waits for them, and re-layouts  13.7 us
    ppermute x10, starting transfers between devices, shift(): return lax.ppermute(value, axis, [(k, (k + by) % n) for k in range(n)])  13.3 us
    gather x4, local copies, waits for them, and re-layouts, body(): own_a, own_d, own_b, own_e = [x[mine, slots] for x in (a, d, b, e)]  11.8 us
  transfers between devices with their start and end apart: 20, of which 7 were waited for; matrix products, arithmetic and copies ran while one was open for 39% of the time, Pallas kernels for 0%

profile of v1, /device:TPU:0, one launch (start us, length us, event | category | flops | bytes accessed | tf_op | source)
XLA Modules:
  0.0 329.6 jit_solution(10624039737499645998)
XLA Ops:
  7.2 3.5 %copy.46 = bf16[12,128,6,128]{3,1,0,2:T(8,128)(2,1)} copy(bf16[12,128,6,128]{3,1,2,0:T(8,128)(2,1)} %param.17) | data formatting | bytes 4718592 | tf_op args[2]
  10.8 3.0 gather_fusion.5
  13.7 3.0 collective-permute-start.1
  18.4 2.3 gather_fusion.6
  22.4 3.0 collective-permute-start
  25.5 3.4 %copy.43 = bf16[12,128,6,128]{3,1,0,2:T(8,128)(2,1)} copy(bf16[12,128,6,128]{3,1,2,0:T(8,128)(2,1)} %param.20) | data formatting | bytes 4718592 | tf_op args[5]
  28.8 2.9 gather_fusion.10
  32.4 3.3 %copy.44 = bf16[12,128,6,128]{3,1,0,2:T(8,128)(2,1)} copy(bf16[12,128,6,128]{3,1,2,0:T(8,128)(2,1)} %param.19) | data formatting | bytes 4718592 | tf_op args[4]
  35.8 2.3 gather_fusion.9
  46.1 3.0 gather_fusion.7
  49.0 2.9 gather_fusion.11
  52.0 3.7 %gather_fusion.1 = f32[6,128,128]{2,1,0:T(8,128)} fusion(f32[12,6,128,128]{3,2,1,0:T(8,128)} %bitcast.238, s32[6]{0:T(128)S(1)} %or_bitcast_fusion), kind=kCustom, calls=%fused_computation.1 | custom fusion | bytes 786480 | tf_op jit(solution)/shard_map/gather | solution.py:171
  55.6 3.7 %gather_fusion.4 = f32[6,128,128]{2,1,0:T(8,128)} fusion(f32[12,6,128,128]{3,2,1,0:T(8,128)} %bitcast.236, s32[6]{0:T(128)S(1)} %or_bitcast_fusion), kind=kCustom, calls=%fused_computation.4 | custom fusion | bytes 786480 | tf_op jit(solution)/shard_map/gather | solution.py:170
  59.9 2.4 gather_fusion.3
  63.5 2.5 gather_fusion.2
  83.0 3.0 gather_fusion.13
  85.9 3.0 gather_fusion.12
  110.6 2.4 collective-permute-start.9
  118.2 6.7 %collective-permute-done.9 = f32[6,128,128]{2,1,0:T(8,128)S(1)} collective-permute-done((f32[6,128,128]{2,1,0:T(8,128)S(1)}, f32[6,128,128]{2,1,0:T(8,128)S(1)}, u32[]{:S(2)}, u32[]{:S(2)}) %collective-permute-start.9) | collective-permute-done | bytes 393248 | tf_op jit(solution)/shard_map/ppermute | solution.py:131
  158.7 24.9 %collective-permute-done.10 = bf16[2,14,128,128]{3,2,1,0:T(8,128)(2,1)} collective-permute-done((bf16[2,14,128,128]{3,2,1,0:T(8,128)(2,1)S(1)}, bf16[2,14,128,128]{3,2,1,0:T(8,128)(2,1)}, u32[]{:S(2)}, u32[]{:S(2)}) %collective-permute-start.10) | collective-permute-done | bytes 917536 | tf_op jit(solution)/shard_map/ppermute | solution.py:154
  183.6 27.9 %collective-permute-done.11 = bf16[2,14,128,128]{3,2,1,0:T(8,128)(2,1)} collective-permute-done((bf16[2,14,128,128]{3,2,1,0:T(8,128)(2,1)S(1)}, bf16[2,14,128,128]{3,2,1,0:T(8,128)(2,1)}, u32[]{:S(2)}, u32[]{:S(2)}) %collective-permute-start.11) | collective-permute-done | bytes 917536 | tf_op jit(solution)/shard_map/ppermute | solution.py:154
  211.5 27.3 %collective-permute-done.12 = bf16[2,14,128,128]{3,2,1,0:T(8,128)(2,1)} collective-permute-done((bf16[2,14,128,128]{3,2,1,0:T(8,128)(2,1)S(1)}, bf16[2,14,128,128]{3,2,1,0:T(8,128)(2,1)}, u32[]{:S(2)}, u32[]{:S(2)}) %collective-permute-start.12) | collective-permute-done | bytes 917536 | tf_op jit(solution)/shard_map/ppermute | solution.py:154
  239.2 2.1 maximum_bitcast_fusion
  241.3 4.9 %broadcast_select_fusion = (f32[12,128,6,128]{3,1,2,0:T(8,128)}, f32[12,128,6,128]{3,1,2,0:T(8,128)}) fusion(f32[128,6,128]{2,0,1:T(8,128)S(1)} %bitcast.240, pred[12,6]{1,0:T(8,128)(4,1)S(1)} %fusion.54, f32[128,6,128]{2,0,1:T(8,128)S(1)} %bitcast.241), kind=kLoop, calls=%fused_computation.30 | loop fusion | flops 2359296 | bytes 10223688 | tf_op jit(solution)/shard_map/jit(_where)/select_n | solution.py:239
  246.2 7.7 %collective-permute-done.14 = bf16[2,14,128,128]{3,2,1,0:T(8,128)(2,1)} collective-permute-done((bf16[2,14,128,128]{3,2,1,0:T(8,128)(2,1)}, bf16[2,14,128,128]{3,2,1,0:T(8,128)(2,1)}, u32[]{:S(2)}, u32[]{:S(2)}) %collective-permute-start.14) | collective-permute-done | bytes 917536 | tf_op jit(solution)/shard_map/ppermute | solution.py:156
  253.9 18.2 %collective-permute-done.15 = bf16[2,14,128,128]{3,2,1,0:T(8,128)(2,1)} collective-permute-done((bf16[2,14,128,128]{3,2,1,0:T(8,128)(2,1)}, bf16[2,14,128,128]{3,2,1,0:T(8,128)(2,1)}, u32[]{:S(2)}, u32[]{:S(2)}) %collective-permute-start.15) | collective-permute-done | bytes 917536 | tf_op jit(solution)/shard_map/ppermute | solution.py:156
  274.2 2.9 pad_maximum_fusion.ad_ref
  277.1 5.5 %pad_maximum_fusion.1.be_ref = bf16[2,2,42,128,128]{4,3,2,1,0:T(8,128)(2,1)} fusion(bf16[1,2,42,128,128]{4,3,2,1,0:T(8,128)(2,1)} %bitcast.58, bf16[1,2,42,128,128]{4,3,2,1,0:T(8,128)(2,1)} %bitcast.57), kind=kLoop, calls=%fused_computation.18 | loop fusion | flops 2752512 | bytes 11010048 | tf_op jit(solution)/shard_map/stack | solution.py:160
  285.2 3.4 %gather_fusion.16 = f32[12,128,128]{2,1,0:T(8,128)} fusion(f32[8,6,128,128]{3,2,1,0:T(8,128)} %bitcast.242, s32[12]{0:T(128)S(1)} %get-tuple-element.34), kind=kCustom, calls=%fused_computation.16 | custom fusion | bytes 1572960 | tf_op jit(solution)/shard_map/gather | solution.py:218
  288.6 3.4 %gather_fusion.15 = f32[12,128,128]{2,1,0:T(8,128)} fusion(f32[8,6,128,128]{3,2,1,0:T(8,128)} %bitcast.243, s32[12]{0:T(128)S(1)} %get-tuple-element.35), kind=kCustom, calls=%fused_computation.15 | custom fusion | bytes 1572960 | tf_op jit(solution)/shard_map/gather | solution.py:218
  292.0 3.4 %gather_fusion.14 = f32[12,128,128]{2,1,0:T(8,128)} fusion(f32[8,6,128,128]{3,2,1,0:T(8,128)} %bitcast.244, s32[12]{0:T(128)S(1)} %fusion.75), kind=kCustom, calls=%fused_computation.14 | custom fusion | bytes 1572960 | tf_op jit(solution)/shard_map/gather | solution.py:218
  301.5 21.2 %update.1 = (f32[12,6,128,128]{3,2,1,0:T(8,128)}, f32[12,6,128,128]{3,2,1,0:T(8,128)}) custom-call(s32[8]{0:T(128)S(1)} %pad_add_fusion.place, f32[12,6,128,128]{3,2,1,0:T(8,128)} %bitcast.237, f32[12,6,128,128]{3,2,1,0:T(8,128)} %bitcast.239, bf16[12,6,128,128]{3,2,1,0:T(8,128)(2,1)S(1)} %bitcast.200, bf16[12,6,128,128]{3,2,1,0:T(8,128)(2,1)S(1)} %bitcast.201, ...), custom_call_target="tpu_custom_call" | custom-call | tf_op jit(solution)/shard_map/update/pallas_call | solution.py:225
  (229 shorter events, 101.6 us)
Async XLA Ops:
  7.2 52.2 %copy-start = (f32[12,128,128]{2,1,0:T(8,128)S(1)}, f32[12,128,128]{2,1,0:T(8,128)}, u32[]{:S(2)}) copy-start(f32[12,128,128]{2,1,0:T(8,128)} %param.21) | copy-start | bytes 2359300
  7.2 275.4 %all-gather.5.cloned.1.call-start = ((), (), s32[]{:S(2)}) async-start(), calls=%async_computation | async-start | bytes 1966080 | tf_op jit(solution)/shard_map/all_gather | solution.py:209
  7.2 9.5 %copy-start.3 = (bf16[12,128,6,128]{3,1,2,0:T(8,128)(2,1)S(1)}, bf16[12,128,6,128]{3,1,2,0:T(8,128)(2,1)}, u32[]{:S(2)}) copy-start(bf16[12,128,6,128]{3,1,2,0:T(8,128)(2,1)} %param.18) | copy-start | bytes 7077892
  13.7 53.2 %collective-permute-start.1 = (bf16[6,128,128]{2,1,0:T(8,128)(2,1)}, bf16[6,128,128]{2,1,0:T(8,128)(2,1)}, u32[]{:S(2)}, u32[]{:S(2)}) collective-permute-start(bf16[6,128,128]{2,1,0:T(8,128)(2,1)} %gather_fusion.5), channel_id=1, source_target_pairs={{0,1},{1,2},{2,3},{3,4},{4,5},{5,6},{6,7},{7,0},{8,9},{9,10},{10,1... | collective-permute-start | bytes 589832 | tf_op jit(solution)/shard_map/ppermute | solution.py:131
  22.4 46.2 %collective-permute-start = (bf16[2,6,128,128]{3,2,1,0:T(8,128)(2,1)}, bf16[2,6,128,128]{3,2,1,0:T(8,128)(2,1)}, u32[]{:S(2)}, u32[]{:S(2)}) collective-permute-start(bf16[2,6,128,128]{3,2,1,0:T(8,128)(2,1)} %pad_maximum_fusion.14), channel_id=1, source_target_pairs={{0,7},{1,0},{2,1},{3,2},{4,3},{5,4},{6,5},{7,6},{8,15},{9,8},{10,9... | collective-permute-start | bytes 1179656 | tf_op jit(solution)/shard_map/ppermute | solution.py:131
  31.8 45.6 %collective-permute-start.3 = (bf16[6,128,128]{2,1,0:T(8,128)(2,1)}, bf16[6,128,128]{2,1,0:T(8,128)(2,1)}, u32[]{:S(2)}, u32[]{:S(2)}) collective-permute-start(bf16[6,128,128]{2,1,0:T(8,128)(2,1)} %gather_fusion.10), channel_id=1, source_target_pairs={{0,24},{8,0},{16,8},{24,16},{1,25},{9,1},{17,9},{25,17},{2,26},{10... | collective-permute-start | bytes 589832 | tf_op jit(solution)/shard_map/ppermute | solution.py:131
  39.7 37.6 %collective-permute-start.2 = (bf16[2,6,128,128]{3,2,1,0:T(8,128)(2,1)}, bf16[2,6,128,128]{3,2,1,0:T(8,128)(2,1)}, u32[]{:S(2)}, u32[]{:S(2)}) collective-permute-start(bf16[2,6,128,128]{3,2,1,0:T(8,128)(2,1)} %pad_maximum_fusion.15), channel_id=1, source_target_pairs={{0,8},{8,16},{16,24},{24,0},{1,9},{9,17},{17,25},{25,1},{2,10},{10... | collective-permute-start | bytes 1179656 | tf_op jit(solution)/shard_map/ppermute | solution.py:131
  42.8 19.6 %copy-start.33 = (f32[12,128]{1,0:T(8,128)S(1)}, f32[12,128]{1,0:T(8,128)}, u32[]{:S(2)}) copy-start(f32[12,128]{1,0:T(8,128)} %param.24) | copy-start | bytes 18436
  63.5 8.5 %copy-start.5 = (f32[6,128,128]{2,1,0:T(8,128)S(1)}, f32[6,128,128]{2,1,0:T(8,128)}, u32[]{:S(2)}) copy-start(f32[6,128,128]{2,1,0:T(8,128)} %gather_fusion.1) | copy-start | bytes 1179652
  66.0 5.6 %copy-start.24 = (bf16[6,128,128]{2,1,0:T(8,128)(2,1)S(1)}, bf16[6,128,128]{2,1,0:T(8,128)(2,1)}, u32[]{:S(2)}) copy-start(bf16[6,128,128]{2,1,0:T(8,128)(2,1)} %gather_fusion.7) | copy-start | bytes 589828
  69.6 4.1 %copy-start.19 = (f32[6,128,128]{2,1,0:T(8,128)S(1)}, f32[6,128,128]{2,1,0:T(8,128)}, u32[]{:S(2)}) copy-start(f32[6,128,128]{2,1,0:T(8,128)} %param.25) | copy-start | bytes 1179652
  76.0 6.3 %copy-start.32 = (bf16[1,2,128,128]{3,2,1,0:T(8,128)(2,1)S(1)}, bf16[1,2,128,128]{3,2,1,0:T(8,128)(2,1)}, u32[]{:S(2)}) copy-start(bf16[1,2,128,128]{3,2,1,0:T(8,128)(2,1)} %slice_bitcast_fusion.41) | copy-start | bytes 196612
  80.4 16.2 %collective-permute-start.4 = (f32[6,128,128]{2,1,0:T(8,128)}, f32[6,128,128]{2,1,0:T(8,128)}, u32[]{:S(2)}, u32[]{:S(2)}) collective-permute-start(f32[6,128,128]{2,1,0:T(8,128)} %convolution_select_fusion.2), channel_id=1, source_target_pairs={{0,24},{8,0},{16,8},{24,16},{1,25},{9,1},{17,9},{25,17},{2,26},{10... | collective-permute-start | bytes 1179656 | tf_op jit(solution)/shard_map/ppermute | solution.py:131
  82.3 13.4 %collective-permute-start.5 = (f32[6,128,128]{2,1,0:T(8,128)}, f32[6,128,128]{2,1,0:T(8,128)}, u32[]{:S(2)}, u32[]{:S(2)}) collective-permute-start(f32[6,128,128]{2,1,0:T(8,128)} %get-tuple-element.26), channel_id=1, source_target_pairs={{0,1},{1,2},{2,3},{3,4},{4,5},{5,6},{6,7},{7,0},{8,9},{9,10},{10,1... | collective-permute-start | bytes 1179656 | tf_op jit(solution)/shard_map/ppermute | solution.py:131
  92.2 21.2 %collective-permute-start.7 = (f32[6,128,128]{2,1,0:T(8,128)}, f32[6,128,128]{2,1,0:T(8,128)S(1)}, u32[]{:S(2)}, u32[]{:S(2)}) collective-permute-start(f32[6,128,128]{2,1,0:T(8,128)} %get-tuple-element.26), channel_id=1, source_target_pairs={{0,2},{1,3},{2,4},{3,5},{4,6},{5,7},{6,0},{7,1},{8,10},{9,11},{10,... | collective-permute-start | bytes 1179656 | tf_op jit(solution)/shard_map/ppermute | solution.py:131
  93.4 19.6 %collective-permute-start.6 = (f32[6,128,128]{2,1,0:T(8,128)}, f32[6,128,128]{2,1,0:T(8,128)S(1)}, u32[]{:S(2)}, u32[]{:S(2)}) collective-permute-start(f32[6,128,128]{2,1,0:T(8,128)} %convolution_select_fusion.2), channel_id=1, source_target_pairs={{0,16},{8,24},{16,0},{24,8},{1,17},{9,25},{17,1},{25,9},{2,18},{10... | collective-permute-start | bytes 1179656 | tf_op jit(solution)/shard_map/ppermute | solution.py:131
  101.5 4.1 %copy-start.6 = (f32[6,128,128]{2,1,0:T(8,128)S(1)}, f32[6,128,128]{2,1,0:T(8,128)}, u32[]{:S(2)}) copy-start(f32[6,128,128]{2,1,0:T(8,128)} %gather_fusion.4) | copy-start | bytes 1179652
  110.5 15.3 %collective-permute-start.8 = (f32[6,128,128]{2,1,0:T(8,128)S(1)}, f32[6,128,128]{2,1,0:T(8,128)S(1)}, u32[]{:S(2)}, u32[]{:S(2)}) collective-permute-start(f32[6,128,128]{2,1,0:T(8,128)S(1)} %convolution_select_fusion.1), channel_id=1, source_target_pairs={{0,24},{8,0},{16,8},{24,16},{1,25},{9,1},{17,9},{25,17},{2,26},{10... | collective-permute-start | bytes 1179656 | tf_op jit(solution)/shard_map/ppermute | solution.py:131
  110.6 14.2 %collective-permute-start.9 = (f32[6,128,128]{2,1,0:T(8,128)S(1)}, f32[6,128,128]{2,1,0:T(8,128)S(1)}, u32[]{:S(2)}, u32[]{:S(2)}) collective-permute-start(f32[6,128,128]{2,1,0:T(8,128)S(1)} %get-tuple-element.28), channel_id=1, source_target_pairs={{0,1},{1,2},{2,3},{3,4},{4,5},{5,6},{6,7},{7,0},{8,9},{9,10},{10,1... | collective-permute-start | bytes 1179656 | tf_op jit(solution)/shard_map/ppermute | solution.py:131
  114.7 10.3 %copy-start.28 = (bf16[6,128,128]{2,1,0:T(8,128)(2,1)S(1)}, bf16[6,128,128]{2,1,0:T(8,128)(2,1)}, u32[]{:S(2)}) copy-start(bf16[6,128,128]{2,1,0:T(8,128)(2,1)} %gather_fusion.13) | copy-start | bytes 589828
  117.0 8.4 %copy-start.23 = (bf16[6,128,128]{2,1,0:T(8,128)(2,1)S(1)}, bf16[6,128,128]{2,1,0:T(8,128)(2,1)}, u32[]{:S(2)}) copy-start(bf16[6,128,128]{2,1,0:T(8,128)(2,1)} %gather_fusion.11) | copy-start | bytes 589828
  133.0 152.3 %all-gather.7.cloned.1.call-start = ((), (), s32[]{:S(2)}) async-start(), calls=%async_computation.1 | async-start | bytes 3538944 | tf_op jit(solution)/shard_map/all_gather | solution.py:210
  143.1 134.0 %collective-permute-start.16 = (bf16[2,42,128,128]{3,2,1,0:T(8,128)(2,1)}, bf16[2,42,128,128]{3,2,1,0:T(8,128)(2,1)}, u32[]{:S(2)}, u32[]{:S(2)}) collective-permute-start(bf16[2,42,128,128]{3,2,1,0:T(8,128)(2,1)} %maximum_dynamic-update-slice_fusion), channel_id=1, source_target_pairs={{0,8},{8,0},{16,24},{24,16},{1,9},{9,1},{17,25},{25,17},{2,10},{10... | collective-permute-start | bytes 8257544 | tf_op jit(solution)/shard_map/ppermute | solution.py:157
  143.7 133.4 %collective-permute-start.17 = (bf16[2,42,128,128]{3,2,1,0:T(8,128)(2,1)}, bf16[2,42,128,128]{3,2,1,0:T(8,128)(2,1)}, u32[]{:S(2)}, u32[]{:S(2)}) collective-permute-start(bf16[2,42,128,128]{3,2,1,0:T(8,128)(2,1)} %maximum_dynamic-update-slice_fusion), channel_id=1, source_target_pairs={{0,24},{8,16},{16,8},{24,0},{1,25},{9,17},{17,9},{25,1},{2,26},{10... | collective-permute-start | bytes 8257544 | tf_op jit(solution)/shard_map/ppermute | solution.py:158
  155.7 83.4 %copy-start.35 = (s32[6]{0:T(128)S(1)}, s32[6]{0:T(128)}, u32[]{:S(2)}) copy-start(s32[6]{0:T(128)} %constant.136.clone) | copy-start | bytes 76
  156.0 27.6 %collective-permute-start.10 = (bf16[2,14,128,128]{3,2,1,0:T(8,128)(2,1)S(1)}, bf16[2,14,128,128]{3,2,1,0:T(8,128)(2,1)}, u32[]{:S(2)}, u32[]{:S(2)}) collective-permute-start(bf16[2,14,128,128]{3,2,1,0:T(8,128)(2,1)S(1)} %get-tuple-element.23), channel_id=1, source_target_pairs={{0,1},{1,0},{2,3},{3,2},{4,5},{5,4},{6,7},{7,6},{8,9},{9,8},{10,11... | collective-permute-start | bytes 2752520 | tf_op jit(solution)/shard_map/ppermute | solution.py:154
  156.6 54.9 %collective-permute-start.11 = (bf16[2,14,128,128]{3,2,1,0:T(8,128)(2,1)S(1)}, bf16[2,14,128,128]{3,2,1,0:T(8,128)(2,1)}, u32[]{:S(2)}, u32[]{:S(2)}) collective-permute-start(bf16[2,14,128,128]{3,2,1,0:T(8,128)(2,1)S(1)} %get-tuple-element.21), channel_id=1, source_target_pairs={{0,1},{1,0},{2,3},{3,2},{4,5},{5,4},{6,7},{7,6},{8,9},{9,8},{10,11... | collective-permute-start | bytes 2752520 | tf_op jit(solution)/shard_map/ppermute | solution.py:154
  158.1 80.7 %collective-permute-start.12 = (bf16[2,14,128,128]{3,2,1,0:T(8,128)(2,1)S(1)}, bf16[2,14,128,128]{3,2,1,0:T(8,128)(2,1)}, u32[]{:S(2)}, u32[]{:S(2)}) collective-permute-start(bf16[2,14,128,128]{3,2,1,0:T(8,128)(2,1)S(1)} %get-tuple-element.22), channel_id=1, source_target_pairs={{0,1},{1,0},{2,3},{3,2},{4,5},{5,4},{6,7},{7,6},{8,9},{9,8},{10,11... | collective-permute-start | bytes 2752520 | tf_op jit(solution)/shard_map/ppermute | solution.py:154
  183.6 62.6 %collective-permute-start.13 = (bf16[2,14,128,128]{3,2,1,0:T(8,128)(2,1)}, bf16[2,14,128,128]{3,2,1,0:T(8,128)(2,1)}, u32[]{:S(2)}, u32[]{:S(2)}) collective-permute-start(bf16[2,14,128,128]{3,2,1,0:T(8,128)(2,1)} %collective-permute-done.10), channel_id=1, source_target_pairs={{0,2},{1,7},{2,4},{3,1},{4,6},{5,3},{6,0},{7,5},{8,10},{9,15},{10,... | collective-permute-start | bytes 2752520 | tf_op jit(solution)/shard_map/ppermute | solution.py:156
  211.5 42.4 %collective-permute-start.14 = (bf16[2,14,128,128]{3,2,1,0:T(8,128)(2,1)}, bf16[2,14,128,128]{3,2,1,0:T(8,128)(2,1)}, u32[]{:S(2)}, u32[]{:S(2)}) collective-permute-start(bf16[2,14,128,128]{3,2,1,0:T(8,128)(2,1)} %collective-permute-done.11), channel_id=1, source_target_pairs={{0,2},{1,7},{2,4},{3,1},{4,6},{5,3},{6,0},{7,5},{8,10},{9,15},{10,... | collective-permute-start | bytes 2752520 | tf_op jit(solution)/shard_map/ppermute | solution.py:156
  238.9 33.3 %collective-permute-start.15 = (bf16[2,14,128,128]{3,2,1,0:T(8,128)(2,1)}, bf16[2,14,128,128]{3,2,1,0:T(8,128)(2,1)}, u32[]{:S(2)}, u32[]{:S(2)}) collective-permute-start(bf16[2,14,128,128]{3,2,1,0:T(8,128)(2,1)} %collective-permute-done.12), channel_id=1, source_target_pairs={{0,2},{1,7},{2,4},{3,1},{4,6},{5,3},{6,0},{7,5},{8,10},{9,15},{10,... | collective-permute-start | bytes 2752520 | tf_op jit(solution)/shard_map/ppermute | solution.py:156
  301.5 21.2 %copy-start.1 = (f32[12,128,128]{2,1,0:T(8,128)S(1)}, f32[12,128,128]{2,1,0:T(8,128)}, u32[]{:S(2)}) copy-start(f32[12,128,128]{2,1,0:T(8,128)} %param.21) | copy-start | bytes 2359300
  (27 other events, 62.9 us)
Sparse Core Ops, SparseCore 0:
  133.1 20.8 all-gather.4
  156.2 116.3 all-gather.6
